TPU v7x, 32 devices: a whole 2x2x4 slice. The times are simulated.
32 devices in a mesh: seq: 8 (over y, x, core), tensor: 4 (over z).
Axes of the slice: x: 2, y: 2, z: 4, core: 2. Of those that a mesh axis runs over, the one named last changes fastest.
Arguments:
- tokens: bfloat16 [5760, 1536], P('seq'), may hold values from -6 to 6
- norm_gain: float32 [1536], replicated, may hold values from 0.1 to 1.9
- w_qkv: bfloat16 [1536, 3, 1536], P(None, None, 'tensor'), may hold values from -8 to 8
- w_out: bfloat16 [1536, 1536], P('tensor'), may hold values from -0.15625 to 0.15625
- post_gain: float32 [1536], replicated, may hold values from 0.1 to 1.9
- w_up: bfloat16 [1536, 6144], P(None, 'tensor'), may hold values from -0.15625 to 0.15625
- w_down: bfloat16 [6144, 1536], P('tensor'), may hold values from -0.078125 to 0.078125
Outputs:
- layer_out: bfloat16 [5760, 1536], P('seq')
All inputs are finite; a program needn't handle non-finite values.
Results may differ from a plain program's by a relative error of at most 0.015.
Values may be sent and summed in bfloat16 or wider, within the bound.
A program may use at most 128 MiB of HBM per device.

v0:
```python
import jax
import jax.numpy as jnp
from jax import lax
from jax.sharding import PartitionSpec as P

HD = 48


def layer_norm(values, gain):
    mean = jnp.mean(values, axis=-1, keepdims=True)
    centred = values - mean
    var = jnp.mean(centred * centred, axis=-1, keepdims=True)
    return centred * lax.rsqrt(var + 1e-05) * gain


def attend_block(carry, queries, key_rows, value_rows, scale):
    peak, total, accum = carry
    heads = queries.shape[1]
    keys = key_rows.reshape(key_rows.shape[0], heads, -1)
    values = value_rows.reshape(value_rows.shape[0], heads, -1)
    scores = jnp.einsum("qhd,khd->hqk", queries, keys, preferred_element_type=jnp.float32) * scale
    fresh = jnp.maximum(peak, jnp.max(scores, axis=-1))
    factor = jnp.exp(peak - fresh)
    weights = jnp.exp(scores - fresh[..., None])
    total = total * factor + jnp.sum(weights, axis=-1)
    accum = accum * factor[..., None] + jnp.einsum(
        "hqk,khd->hqd", weights.astype(jnp.bfloat16), values, preferred_element_type=jnp.float32
    )
    return (fresh, total, accum)


def empty_state(rows, heads, width):
    return (
        jnp.full((heads, rows), -1e30, jnp.float32),
        jnp.zeros((heads, rows), jnp.float32),
        jnp.zeros((heads, rows, width), jnp.float32),
    )


def per_device(tokens, norm_gain, w_qkv, w_out, post_gain, w_up, w_down):
    rows = tokens.shape[0]
    local_heads = w_qkv.shape[2] // HD
    scale = 1.0 / HD**0.5
    base = tokens.astype(jnp.float32)
    normed = layer_norm(base, norm_gain).astype(jnp.bfloat16)
    qkv = jnp.dot(
        normed, w_qkv.reshape(w_qkv.shape[0], -1), preferred_element_type=jnp.float32
    ).astype(jnp.bfloat16)
    span = local_heads * HD
    query = qkv[:, :span]
    key = qkv[:, span : 2 * span]
    value = qkv[:, 2 * span :]
    query3 = query.reshape(rows, local_heads, HD)
    key_piece = lax.all_gather(key, "seq", axis=0, tiled=True)
    value_piece = lax.all_gather(value, "seq", axis=0, tiled=True)
    count = key_piece.shape[0]
    block = count
    while block > 1024 and block % 2 == 0:
        block = block // 2

    def step(index, state):
        first = index * block
        key_block = lax.dynamic_slice_in_dim(key_piece, first, block, 0)
        value_block = lax.dynamic_slice_in_dim(value_piece, first, block, 0)
        return attend_block(state, query3, key_block, value_block, scale)

    peak, total, accum = lax.fori_loop(0, count // block, step, empty_state(rows, local_heads, HD))
    result = accum / total[..., None]
    attended = jnp.transpose(result, (1, 0, 2)).reshape(rows, span).astype(jnp.bfloat16)
    attn_term = jnp.dot(attended, w_out, preferred_element_type=jnp.float32)
    mixed = base + lax.psum(attn_term.astype(jnp.bfloat16), "tensor").astype(jnp.float32)
    post = layer_norm(mixed, post_gain).astype(jnp.bfloat16)
    hidden = jax.nn.gelu(
        jnp.dot(post, w_up, preferred_element_type=jnp.float32), approximate=True
    ).astype(jnp.bfloat16)
    mlp_term = jnp.dot(hidden, w_down, preferred_element_type=jnp.float32)
    return (mixed + lax.psum(mlp_term.astype(jnp.bfloat16), "tensor").astype(jnp.float32)).astype(
        jnp.bfloat16
    )


def solution(mesh):
    placed = (
        P("seq", None),
        P(),
        P(None, None, "tensor"),
        P("tensor", None),
        P(),
        P(None, "tensor"),
        P("tensor", None),
    )
    return jax.shard_map(
        per_device, mesh=mesh, in_specs=placed, out_specs=P("seq", None), check_vma=False
    )
```

profile of v0, /device:TPU:0, one launch (start us, length us, event | category | flops | bytes accessed | tf_op | source)
XLA Modules:
  0.0 578.7 jit_solution(9343756593150286933)
XLA Ops:
  11.1 6.1 %copy.13 = bf16[1536,3,384]{0,2,1:T(8,128)(2,1)} copy(bf16[1536,3,384]{2,0,1:T(8,128)(2,1)} %param.11) | data formatting | bytes 7077888 | tf_op args[2]
  17.3 5.1 convolution_convert_fusion.2
  24.9 39.2 %all-gather.5.cloned.1.call-done = bf16[5760,384]{1,0:T(8,128)(2,1)} async-done(((bf16[720,384]{1,0:T(8,128)(2,1)}), bf16[5760,384]{1,0:T(8,128)(2,1)}) %all-gather.5.cloned.1.call-update) | async-done | bytes 4423696 | tf_op jit(solution)/shard_map/all_gather | solution.py:55
  64.0 39.5 %all-gather.3.cloned.1.call-done = bf16[5760,384]{1,0:T(8,128)(2,1)} async-done(((bf16[720,384]{1,0:T(8,128)(2,1)}), bf16[5760,384]{1,0:T(8,128)(2,1)}) %all-gather.3.cloned.1.call-update) | async-done | bytes 4423696 | tf_op jit(solution)/shard_map/all_gather | solution.py:54
  103.5 264.1 %while.18 = (s32[]{:T(128)}, f32[8,720]{1,0:T(8,128)}, f32[8,720]{1,0:T(8,128)}, f32[8,720,48]{1,2,0:T(8,128)}, bf16[5760,384]{1,0:T(8,128)(2,1)}, /*index=5*/bf...) while((s32[]{:T(128)}, f32[8,720]{1,0:T(8,128)}, ...), condition=%wide.region_5.0_spmd.clone, body=%wide.region_2.0_spmd.clone.sunk | while | flops 830298240 | bytes 67369216 | solution.py:67
  105.3 8.6 %bitcast_reduce_fusion.2 = (f32[8,720]{1,0:T(8,128)S(1)}, f32[8,720,720]{2,1,0:T(8,128)}) fusion(bf16[720,8,48]{0,2,1:T(8,128)(2,1)S(1)} %bitcast.44, bf16[720,8,48]{0,2,1:T(8,128)(2,1)S(1)} %get-tuple-element.275), kind=kOutput, calls=%fused_computation.1.clone.1 | convolution fusion | flops 406419840 | bytes 17717760 | tf_op jit(solution)/shard_map/while/body/eval_jaxpr/qhd,khd->hqk/dot_general | solution.py:21
  114.5 9.7 %fusion.56 = f32[8,720]{1,0:T(8,128)} fusion(f32[8,720,720]{2,1,0:T(8,128)} %get-tuple-element.244, f32[8,720]{1,0:T(8,128)} %select_maximum_fusion.2), kind=kLoop, calls=%fused_computation.4.clone.1 | loop fusion | flops 12435840 | bytes 16634880 | tf_op jit(solution)/shard_map/while/body/eval_jaxpr/reduce_sum | solution.py:25
  125.6 9.2 %fusion.58 = f32[8,720,48]{1,2,0:T(8,128)S(1)} fusion(bf16[720,8,48]{0,2,1:T(8,128)(2,1)S(1)} %bitcast.43, f32[8,720,720]{2,1,0:T(8,128)} %get-tuple-element.244, f32[8,720]{1,0:T(8,128)} %select_maximum_fusion.2, f32[8,720,48]{1,2,0:T(8,128)S(1)} %copy-done.3, f32[8,720]{1,0:T(8,128)S(1)} %get-tuple-element.247, pred[]{:T(512)S(6)} %compare.3), kind=kOutput, calls=%fused_computation.6.clone.1 | convolution fusion | flops 411402240 | bytes 19399680 | tf_op jit(solution)/shard_map/while/body/eval_jaxpr/hqk,khd->hqd/dot_general | solution.py:26
  137.7 8.6 %bitcast_reduce_fusion.2 = (f32[8,720]{1,0:T(8,128)S(1)}, f32[8,720,720]{2,1,0:T(8,128)}) fusion(bf16[720,8,48]{0,2,1:T(8,128)(2,1)S(1)} %bitcast.44, bf16[720,8,48]{0,2,1:T(8,128)(2,1)S(1)} %get-tuple-element.275), kind=kOutput, calls=%fused_computation.1.clone.1 | convolution fusion | flops 406419840 | bytes 17717760 | tf_op jit(solution)/shard_map/while/body/eval_jaxpr/qhd,khd->hqk/dot_general | solution.py:21
  147.6 9.7 %fusion.56 = f32[8,720]{1,0:T(8,128)} fusion(f32[8,720,720]{2,1,0:T(8,128)} %get-tuple-element.244, f32[8,720]{1,0:T(8,128)} %select_maximum_fusion.2), kind=kLoop, calls=%fused_computation.4.clone.1 | loop fusion | flops 12435840 | bytes 16634880 | tf_op jit(solution)/shard_map/while/body/eval_jaxpr/reduce_sum | solution.py:25
  158.7 9.2 %fusion.58 = f32[8,720,48]{1,2,0:T(8,128)S(1)} fusion(bf16[720,8,48]{0,2,1:T(8,128)(2,1)S(1)} %bitcast.43, f32[8,720,720]{2,1,0:T(8,128)} %get-tuple-element.244, f32[8,720]{1,0:T(8,128)} %select_maximum_fusion.2, f32[8,720,48]{1,2,0:T(8,128)S(1)} %copy-done.3, f32[8,720]{1,0:T(8,128)S(1)} %get-tuple-element.247, pred[]{:T(512)S(6)} %compare.3), kind=kOutput, calls=%fused_computation.6.clone.1 | convolution fusion | flops 411402240 | bytes 19399680 | tf_op jit(solution)/shard_map/while/body/eval_jaxpr/hqk,khd->hqd/dot_general | solution.py:26
  170.8 8.6 %bitcast_reduce_fusion.2 = (f32[8,720]{1,0:T(8,128)S(1)}, f32[8,720,720]{2,1,0:T(8,128)}) fusion(bf16[720,8,48]{0,2,1:T(8,128)(2,1)S(1)} %bitcast.44, bf16[720,8,48]{0,2,1:T(8,128)(2,1)S(1)} %get-tuple-element.275), kind=kOutput, calls=%fused_computation.1.clone.1 | convolution fusion | flops 406419840 | bytes 17717760 | tf_op jit(solution)/shard_map/while/body/eval_jaxpr/qhd,khd->hqk/dot_general | solution.py:21
  180.7 9.7 %fusion.56 = f32[8,720]{1,0:T(8,128)} fusion(f32[8,720,720]{2,1,0:T(8,128)} %get-tuple-element.244, f32[8,720]{1,0:T(8,128)} %select_maximum_fusion.2), kind=kLoop, calls=%fused_computation.4.clone.1 | loop fusion | flops 12435840 | bytes 16634880 | tf_op jit(solution)/shard_map/while/body/eval_jaxpr/reduce_sum | solution.py:25
  191.9 9.2 %fusion.58 = f32[8,720,48]{1,2,0:T(8,128)S(1)} fusion(bf16[720,8,48]{0,2,1:T(8,128)(2,1)S(1)} %bitcast.43, f32[8,720,720]{2,1,0:T(8,128)} %get-tuple-element.244, f32[8,720]{1,0:T(8,128)} %select_maximum_fusion.2, f32[8,720,48]{1,2,0:T(8,128)S(1)} %copy-done.3, f32[8,720]{1,0:T(8,128)S(1)} %get-tuple-element.247, pred[]{:T(512)S(6)} %compare.3), kind=kOutput, calls=%fused_computation.6.clone.1 | convolution fusion | flops 411402240 | bytes 19399680 | tf_op jit(solution)/shard_map/while/body/eval_jaxpr/hqk,khd->hqd/dot_general | solution.py:26
  203.9 8.6 %bitcast_reduce_fusion.2 = (f32[8,720]{1,0:T(8,128)S(1)}, f32[8,720,720]{2,1,0:T(8,128)}) fusion(bf16[720,8,48]{0,2,1:T(8,128)(2,1)S(1)} %bitcast.44, bf16[720,8,48]{0,2,1:T(8,128)(2,1)S(1)} %get-tuple-element.275), kind=kOutput, calls=%fused_computation.1.clone.1 | convolution fusion | flops 406419840 | bytes 17717760 | tf_op jit(solution)/shard_map/while/body/eval_jaxpr/qhd,khd->hqk/dot_general | solution.py:21
  213.8 9.7 %fusion.56 = f32[8,720]{1,0:T(8,128)} fusion(f32[8,720,720]{2,1,0:T(8,128)} %get-tuple-element.244, f32[8,720]{1,0:T(8,128)} %select_maximum_fusion.2), kind=kLoop, calls=%fused_computation.4.clone.1 | loop fusion | flops 12435840 | bytes 16634880 | tf_op jit(solution)/shard_map/while/body/eval_jaxpr/reduce_sum | solution.py:25
  225.0 9.2 %fusion.58 = f32[8,720,48]{1,2,0:T(8,128)S(1)} fusion(bf16[720,8,48]{0,2,1:T(8,128)(2,1)S(1)} %bitcast.43, f32[8,720,720]{2,1,0:T(8,128)} %get-tuple-element.244, f32[8,720]{1,0:T(8,128)} %select_maximum_fusion.2, f32[8,720,48]{1,2,0:T(8,128)S(1)} %copy-done.3, f32[8,720]{1,0:T(8,128)S(1)} %get-tuple-element.247, pred[]{:T(512)S(6)} %compare.3), kind=kOutput, calls=%fused_computation.6.clone.1 | convolution fusion | flops 411402240 | bytes 19399680 | tf_op jit(solution)/shard_map/while/body/eval_jaxpr/hqk,khd->hqd/dot_general | solution.py:26
  237.0 8.6 %bitcast_reduce_fusion.2 = (f32[8,720]{1,0:T(8,128)S(1)}, f32[8,720,720]{2,1,0:T(8,128)}) fusion(bf16[720,8,48]{0,2,1:T(8,128)(2,1)S(1)} %bitcast.44, bf16[720,8,48]{0,2,1:T(8,128)(2,1)S(1)} %get-tuple-element.275), kind=kOutput, calls=%fused_computation.1.clone.1 | convolution fusion | flops 406419840 | bytes 17717760 | tf_op jit(solution)/shard_map/while/body/eval_jaxpr/qhd,khd->hqk/dot_general | solution.py:21
  246.9 9.7 %fusion.56 = f32[8,720]{1,0:T(8,128)} fusion(f32[8,720,720]{2,1,0:T(8,128)} %get-tuple-element.244, f32[8,720]{1,0:T(8,128)} %select_maximum_fusion.2), kind=kLoop, calls=%fused_computation.4.clone.1 | loop fusion | flops 12435840 | bytes 16634880 | tf_op jit(solution)/shard_map/while/body/eval_jaxpr/reduce_sum | solution.py:25
  258.1 9.2 %fusion.58 = f32[8,720,48]{1,2,0:T(8,128)S(1)} fusion(bf16[720,8,48]{0,2,1:T(8,128)(2,1)S(1)} %bitcast.43, f32[8,720,720]{2,1,0:T(8,128)} %get-tuple-element.244, f32[8,720]{1,0:T(8,128)} %select_maximum_fusion.2, f32[8,720,48]{1,2,0:T(8,128)S(1)} %copy-done.3, f32[8,720]{1,0:T(8,128)S(1)} %get-tuple-element.247, pred[]{:T(512)S(6)} %compare.3), kind=kOutput, calls=%fused_computation.6.clone.1 | convolution fusion | flops 411402240 | bytes 19399680 | tf_op jit(solution)/shard_map/while/body/eval_jaxpr/hqk,khd->hqd/dot_general | solution.py:26
  270.1 8.6 %bitcast_reduce_fusion.2 = (f32[8,720]{1,0:T(8,128)S(1)}, f32[8,720,720]{2,1,0:T(8,128)}) fusion(bf16[720,8,48]{0,2,1:T(8,128)(2,1)S(1)} %bitcast.44, bf16[720,8,48]{0,2,1:T(8,128)(2,1)S(1)} %get-tuple-element.275), kind=kOutput, calls=%fused_computation.1.clone.1 | convolution fusion | flops 406419840 | bytes 17717760 | tf_op jit(solution)/shard_map/while/body/eval_jaxpr/qhd,khd->hqk/dot_general | solution.py:21
  280.0 9.7 %fusion.56 = f32[8,720]{1,0:T(8,128)} fusion(f32[8,720,720]{2,1,0:T(8,128)} %get-tuple-element.244, f32[8,720]{1,0:T(8,128)} %select_maximum_fusion.2), kind=kLoop, calls=%fused_computation.4.clone.1 | loop fusion | flops 12435840 | bytes 16634880 | tf_op jit(solution)/shard_map/while/body/eval_jaxpr/reduce_sum | solution.py:25
  291.2 9.2 %fusion.58 = f32[8,720,48]{1,2,0:T(8,128)S(1)} fusion(bf16[720,8,48]{0,2,1:T(8,128)(2,1)S(1)} %bitcast.43, f32[8,720,720]{2,1,0:T(8,128)} %get-tuple-element.244, f32[8,720]{1,0:T(8,128)} %select_maximum_fusion.2, f32[8,720,48]{1,2,0:T(8,128)S(1)} %copy-done.3, f32[8,720]{1,0:T(8,128)S(1)} %get-tuple-element.247, pred[]{:T(512)S(6)} %compare.3), kind=kOutput, calls=%fused_computation.6.clone.1 | convolution fusion | flops 411402240 | bytes 19399680 | tf_op jit(solution)/shard_map/while/body/eval_jaxpr/hqk,khd->hqd/dot_general | solution.py:26
  303.2 8.6 %bitcast_reduce_fusion.2 = (f32[8,720]{1,0:T(8,128)S(1)}, f32[8,720,720]{2,1,0:T(8,128)}) fusion(bf16[720,8,48]{0,2,1:T(8,128)(2,1)S(1)} %bitcast.44, bf16[720,8,48]{0,2,1:T(8,128)(2,1)S(1)} %get-tuple-element.275), kind=kOutput, calls=%fused_computation.1.clone.1 | convolution fusion | flops 406419840 | bytes 17717760 | tf_op jit(solution)/shard_map/while/body/eval_jaxpr/qhd,khd->hqk/dot_general | solution.py:21
  313.1 9.7 %fusion.56 = f32[8,720]{1,0:T(8,128)} fusion(f32[8,720,720]{2,1,0:T(8,128)} %get-tuple-element.244, f32[8,720]{1,0:T(8,128)} %select_maximum_fusion.2), kind=kLoop, calls=%fused_computation.4.clone.1 | loop fusion | flops 12435840 | bytes 16634880 | tf_op jit(solution)/shard_map/while/body/eval_jaxpr/reduce_sum | solution.py:25
  324.3 9.2 %fusion.58 = f32[8,720,48]{1,2,0:T(8,128)S(1)} fusion(bf16[720,8,48]{0,2,1:T(8,128)(2,1)S(1)} %bitcast.43, f32[8,720,720]{2,1,0:T(8,128)} %get-tuple-element.244, f32[8,720]{1,0:T(8,128)} %select_maximum_fusion.2, f32[8,720,48]{1,2,0:T(8,128)S(1)} %copy-done.3, f32[8,720]{1,0:T(8,128)S(1)} %get-tuple-element.247, pred[]{:T(512)S(6)} %compare.3), kind=kOutput, calls=%fused_computation.6.clone.1 | convolution fusion | flops 411402240 | bytes 19399680 | tf_op jit(solution)/shard_map/while/body/eval_jaxpr/hqk,khd->hqd/dot_general | solution.py:26
  336.3 8.6 %bitcast_reduce_fusion.2 = (f32[8,720]{1,0:T(8,128)S(1)}, f32[8,720,720]{2,1,0:T(8,128)}) fusion(bf16[720,8,48]{0,2,1:T(8,128)(2,1)S(1)} %bitcast.44, bf16[720,8,48]{0,2,1:T(8,128)(2,1)S(1)} %get-tuple-element.275), kind=kOutput, calls=%fused_computation.1.clone.1 | convolution fusion | flops 406419840 | bytes 17717760 | tf_op jit(solution)/shard_map/while/body/eval_jaxpr/qhd,khd->hqk/dot_general | solution.py:21
  346.2 9.7 %fusion.56 = f32[8,720]{1,0:T(8,128)} fusion(f32[8,720,720]{2,1,0:T(8,128)} %get-tuple-element.244, f32[8,720]{1,0:T(8,128)} %select_maximum_fusion.2), kind=kLoop, calls=%fused_computation.4.clone.1 | loop fusion | flops 12435840 | bytes 16634880 | tf_op jit(solution)/shard_map/while/body/eval_jaxpr/reduce_sum | solution.py:25
  357.4 9.2 %fusion.58 = f32[8,720,48]{1,2,0:T(8,128)S(1)} fusion(bf16[720,8,48]{0,2,1:T(8,128)(2,1)S(1)} %bitcast.43, f32[8,720,720]{2,1,0:T(8,128)} %get-tuple-element.244, f32[8,720]{1,0:T(8,128)} %select_maximum_fusion.2, f32[8,720,48]{1,2,0:T(8,128)S(1)} %copy-done.3, f32[8,720]{1,0:T(8,128)S(1)} %get-tuple-element.247, pred[]{:T(512)S(6)} %compare.3), kind=kOutput, calls=%fused_computation.6.clone.1 | convolution fusion | flops 411402240 | bytes 19399680 | tf_op jit(solution)/shard_map/while/body/eval_jaxpr/hqk,khd->hqd/dot_general | solution.py:26
  372.0 90.0 %all-reduce.3.cloned.1.call-done = bf16[720,1536]{1,0:T(8,128)(2,1)} async-done(((bf16[720,1536]{1,0:T(8,128)(2,1)}), bf16[720,1536]{1,0:T(8,128)(2,1)}) %all-reduce.3.cloned.1.call-update) | async-done | bytes 2211856 | tf_op jit(solution)/shard_map/psum | solution.py:71
  465.4 12.9 %convolution_convert_fusion = bf16[720,1536]{1,0:T(8,128)(2,1)} fusion(bf16[1536,1536]{1,0:T(8,128)(2,1)} %param.15, bf16[1536,1536]{1,0:T(8,128)(2,1)} %param.14, bf16[720,1536]{1,0:T(8,128)(2,1)} %all-reduce.3.cloned.1.call-done, bf16[720,1536]{1,0:T(8,128)(2,1)S(1)} %copy-done.2, f32[1536]{0:T(1024)S(1)} %copy-done.8, f32[720]{0:T(1024)S(1)} %add_rsqrt_fusion, ...), kind=kOutput, calls=%fused_computation.36 | convolution fusion | flops 6813573120 | bytes 16084608 | tf_op jit(solution)/shard_map/dot_general | solution.py:76
  478.4 89.3 %all-reduce.5.cloned.1.call-done = bf16[720,1536]{1,0:T(8,128)(2,1)} async-done(((bf16[720,1536]{1,0:T(8,128)(2,1)}), bf16[720,1536]{1,0:T(8,128)(2,1)}) %all-reduce.5.cloned.1.call-update) | async-done | bytes 2211856 | tf_op jit(solution)/shard_map/psum | solution.py:77
  (132 shorter events, 63.4 us)
Async XLA Ops:
  6.5 362.4 %copy-start = (bf16[384,1536]{1,0:T(8,128)(2,1)S(1)}, bf16[384,1536]{1,0:T(8,128)(2,1)}, u32[]{:S(2)}) copy-start(bf16[384,1536]{1,0:T(8,128)(2,1)} %param.12) | copy-start | bytes 3538948
  6.5 57.5 %all-gather.5.cloned.1.call-start = ((), (), s32[]{:S(2)}) async-start(), calls=%async_computation.1 | async-start | bytes 4976640 | tf_op jit(solution)/shard_map/all_gather | solution.py:55
  8.6 8.6 %copy-start.1 = (bf16[720,1536]{1,0:T(8,128)(2,1)S(1)}, bf16[720,1536]{1,0:T(8,128)(2,1)}, u32[]{:S(2)}) copy-start(bf16[720,1536]{1,0:T(8,128)(2,1)} %param.9) | copy-start | bytes 6635524
  8.6 8.6 %copy-start.7 = (f32[1536]{0:T(1024)S(1)}, f32[1536]{0:T(1024)}, u32[]{:S(2)}) copy-start(f32[1536]{0:T(1024)} %param.10) | copy-start | bytes 18436
  23.6 79.9 %all-gather.3.cloned.1.call-start = ((), (), s32[]{:S(2)}) async-start(), calls=%async_computation | async-start | bytes 4976640 | tf_op jit(solution)/shard_map/all_gather | solution.py:54
  24.3 437.7 %all-reduce.3.cloned.1.call-start = ((), (), s32[]{:S(2)}) async-start(), calls=%async_computation.2 | async-start | bytes 4423680 | tf_op jit(solution)/shard_map/psum | solution.py:71
  114.5 11.1 %copy-start.3 = (f32[8,720,48]{1,2,0:T(8,128)S(1)}, f32[8,720,48]{1,2,0:T(8,128)}, u32[]{:S(2)}) copy-start(f32[8,720,48]{1,2,0:T(8,128)} %get-tuple-element.262) | copy-start | bytes 3317764 | tf_op jit(solution)/shard_map/while
  125.6 9.2 %copy-start.6 = (f32[8,720]{1,0:T(8,128)S(1)}, f32[8,720]{1,0:T(8,128)}, u32[]{:S(2)}) copy-start(f32[8,720]{1,0:T(8,128)} %select_maximum_fusion.2) | copy-start | bytes 69124 | tf_op jit(solution)/shard_map/while
  134.8 1.0 copy-start.4
  147.6 11.2 %copy-start.3 = (f32[8,720,48]{1,2,0:T(8,128)S(1)}, f32[8,720,48]{1,2,0:T(8,128)}, u32[]{:S(2)}) copy-start(f32[8,720,48]{1,2,0:T(8,128)} %get-tuple-element.262) | copy-start | bytes 3317764 | tf_op jit(solution)/shard_map/while
  158.7 9.2 %copy-start.6 = (f32[8,720]{1,0:T(8,128)S(1)}, f32[8,720]{1,0:T(8,128)}, u32[]{:S(2)}) copy-start(f32[8,720]{1,0:T(8,128)} %select_maximum_fusion.2) | copy-start | bytes 69124 | tf_op jit(solution)/shard_map/while
  167.9 1.0 copy-start.4
  180.7 11.2 %copy-start.3 = (f32[8,720,48]{1,2,0:T(8,128)S(1)}, f32[8,720,48]{1,2,0:T(8,128)}, u32[]{:S(2)}) copy-start(f32[8,720,48]{1,2,0:T(8,128)} %get-tuple-element.262) | copy-start | bytes 3317764 | tf_op jit(solution)/shard_map/while
  191.8 9.2 %copy-start.6 = (f32[8,720]{1,0:T(8,128)S(1)}, f32[8,720]{1,0:T(8,128)}, u32[]{:S(2)}) copy-start(f32[8,720]{1,0:T(8,128)} %select_maximum_fusion.2) | copy-start | bytes 69124 | tf_op jit(solution)/shard_map/while
  213.8 11.2 %copy-start.3 = (f32[8,720,48]{1,2,0:T(8,128)S(1)}, f32[8,720,48]{1,2,0:T(8,128)}, u32[]{:S(2)}) copy-start(f32[8,720,48]{1,2,0:T(8,128)} %get-tuple-element.262) | copy-start | bytes 3317764 | tf_op jit(solution)/shard_map/while
  225.0 9.2 %copy-start.6 = (f32[8,720]{1,0:T(8,128)S(1)}, f32[8,720]{1,0:T(8,128)}, u32[]{:S(2)}) copy-start(f32[8,720]{1,0:T(8,128)} %select_maximum_fusion.2) | copy-start | bytes 69124 | tf_op jit(solution)/shard_map/while
  246.9 11.2 %copy-start.3 = (f32[8,720,48]{1,2,0:T(8,128)S(1)}, f32[8,720,48]{1,2,0:T(8,128)}, u32[]{:S(2)}) copy-start(f32[8,720,48]{1,2,0:T(8,128)} %get-tuple-element.262) | copy-start | bytes 3317764 | tf_op jit(solution)/shard_map/while
  258.1 9.2 %copy-start.6 = (f32[8,720]{1,0:T(8,128)S(1)}, f32[8,720]{1,0:T(8,128)}, u32[]{:S(2)}) copy-start(f32[8,720]{1,0:T(8,128)} %select_maximum_fusion.2) | copy-start | bytes 69124 | tf_op jit(solution)/shard_map/while
  267.2 1.0 copy-start.4
  280.0 11.2 %copy-start.3 = (f32[8,720,48]{1,2,0:T(8,128)S(1)}, f32[8,720,48]{1,2,0:T(8,128)}, u32[]{:S(2)}) copy-start(f32[8,720,48]{1,2,0:T(8,128)} %get-tuple-element.262) | copy-start | bytes 3317764 | tf_op jit(solution)/shard_map/while
  291.2 9.2 %copy-start.6 = (f32[8,720]{1,0:T(8,128)S(1)}, f32[8,720]{1,0:T(8,128)}, u32[]{:S(2)}) copy-start(f32[8,720]{1,0:T(8,128)} %select_maximum_fusion.2) | copy-start | bytes 69124 | tf_op jit(solution)/shard_map/while
  300.4 1.0 copy-start.4
  313.1 11.2 %copy-start.3 = (f32[8,720,48]{1,2,0:T(8,128)S(1)}, f32[8,720,48]{1,2,0:T(8,128)}, u32[]{:S(2)}) copy-start(f32[8,720,48]{1,2,0:T(8,128)} %get-tuple-element.262) | copy-start | bytes 3317764 | tf_op jit(solution)/shard_map/while
  324.3 9.2 %copy-start.6 = (f32[8,720]{1,0:T(8,128)S(1)}, f32[8,720]{1,0:T(8,128)}, u32[]{:S(2)}) copy-start(f32[8,720]{1,0:T(8,128)} %select_maximum_fusion.2) | copy-start | bytes 69124 | tf_op jit(solution)/shard_map/while
  333.5 1.0 copy-start.4
  346.2 11.2 %copy-start.3 = (f32[8,720,48]{1,2,0:T(8,128)S(1)}, f32[8,720,48]{1,2,0:T(8,128)}, u32[]{:S(2)}) copy-start(f32[8,720,48]{1,2,0:T(8,128)} %get-tuple-element.262) | copy-start | bytes 3317764 | tf_op jit(solution)/shard_map/while
  357.4 9.2 %copy-start.6 = (f32[8,720]{1,0:T(8,128)S(1)}, f32[8,720]{1,0:T(8,128)}, u32[]{:S(2)}) copy-start(f32[8,720]{1,0:T(8,128)} %select_maximum_fusion.2) | copy-start | bytes 69124 | tf_op jit(solution)/shard_map/while
  366.6 1.0 copy-start.4
  369.0 93.0 %copy-start.2 = (bf16[720,1536]{1,0:T(8,128)(2,1)S(1)}, bf16[720,1536]{1,0:T(8,128)(2,1)}, u32[]{:S(2)}) copy-start(bf16[720,1536]{1,0:T(8,128)(2,1)} %param.9) | copy-start | bytes 6635524
  371.7 93.7 %copy-start.8 = (f32[1536]{0:T(1024)S(1)}, f32[1536]{0:T(1024)}, u32[]{:S(2)}) copy-start(f32[1536]{0:T(1024)} %param.13) | copy-start | bytes 18436
  371.7 196.0 %all-reduce.5.cloned.1.call-start = ((), (), s32[]{:S(2)}) async-start(), calls=%async_computation.3 | async-start | bytes 4423680 | tf_op jit(solution)/shard_map/psum | solution.py:77
  462.0 2.4 copy-start.5
  (2 other events, 2.0 us)
Sparse Core Ops, SparseCore 0:
  23.7 40.2 all-gather.4
  65.9 37.5 all-gather.2
  371.8 90.1 all-reduce.2
  478.5 89.1 all-reduce.4
where the time goes:
time: 580 us; the launch traced here: 579 us
  waiting for transfers between devices  259 us (45%)
  matrix products  163 us (28%)
  other arithmetic  113 us (19%)
  local copies, waits for them, and re-layouts  30.3 us (5%)
  between operations  13.2 us (2%)
    psum x1, waiting for transfers between devices, per_device(): lax.psum(attn_term.astype(jnp.bfloat16), 'tensor').astype(jnp.float32)  90 us
    psum x1, waiting for transfers between devices, per_device(): lax.psum(mlp_term.astype(jnp.bfloat16), 'tensor').astype(jnp.float32)  89.3 us
    reduce_sum x8, other arithmetic, attend_block(): total = total * factor + jnp.sum(weights, axis=-1)  77.9 us
    dot_general x8, matrix products, attend_block(): jnp.einsum('hqk,khd->hqd', weights.astype(jnp.bfloat16), values, preferre...  73.3 us
    dot_general x8, matrix products, attend_block(): jnp.einsum('qhd,khd->hqk', queries, keys, preferred_element_type=jnp.floa...  68.5 us
    all_gather x1, waiting for transfers between devices, per_device(): key_piece = lax.all_gather(key, 'seq', axis=0, tiled=True)  39.5 us
    all_gather x1, waiting for transfers between devices, per_device(): value_piece = lax.all_gather(value, 'seq', axis=0, tiled=True)  39.2 us
    dot_general x1, matrix products, per_device(): mlp_term = jnp.dot(hidden, w_down, preferred_element_type=jnp.float32)  12.9 us
  transfers between devices with their start and end apart: 4, of which 4 were waited for; matrix products, arithmetic and copies ran while one was open for 0% of the time, Pallas kernels for 0%

commit v1 on v0

--- a/solution.py
+++ b/solution.py
@@ -74,9 +74,12 @@
         jnp.dot(post, w_up, preferred_element_type=jnp.float32), approximate=True
     ).astype(jnp.bfloat16)
     mlp_term = jnp.dot(hidden, w_down, preferred_element_type=jnp.float32)
-    return (mixed + lax.psum(mlp_term.astype(jnp.bfloat16), "tensor").astype(jnp.float32)).astype(
-        jnp.bfloat16
-    )
+    return (
+        mixed
+        + jnp.sum(lax.all_gather(mlp_term.astype(jnp.bfloat16), "tensor"), axis=0).astype(
+            jnp.float32
+        )
+    ).astype(jnp.bfloat16)
 
 
 def solution(mesh):

time: 580 us -> 654 us (1.13)
  waiting for transfers between devices: 259 us -> 326 us
  other arithmetic: 113 us -> 120 us
    all_gather x0 -> x1, waiting for transfers between devices: none -> 156 us  [per_device(): lax.all_gather(mlp_term.astype(jnp.bfloat16), 'tensor')]
    psum x1 -> x0, waiting for transfers between devices: 89.3 us -> none  [per_device(): lax.psum(mlp_term.astype(jnp.bfloat16), 'tensor').astype(jnp.float32)]
    reduce_sum x0 -> x1, other arithmetic: none -> 6.89 us  [per_device(): jnp.sum(lax.all_gather(mlp_term.astype(jnp.bfloat16), 'tensor'), axis=0)]
where the time goes in v1:
time: 654 us; the launch traced here: 653 us
  waiting for transfers between devices  326 us (50%)
  matrix products  163 us (25%)
  other arithmetic  120 us (18%)
  local copies, waits for them, and re-layouts  30.3 us (5%)
  between operations  13.2 us (2%)
    all_gather x1, waiting for transfers between devices, per_device(): lax.all_gather(mlp_term.astype(jnp.bfloat16), 'tensor')  156 us
    psum x1, waiting for transfers between devices, per_device(): lax.psum(attn_term.astype(jnp.bfloat16), 'tensor').astype(jnp.float32)  90 us
    reduce_sum x8, other arithmetic, attend_block(): total = total * factor + jnp.sum(weights, axis=-1)  77.9 us
    dot_general x8, matrix products, attend_block(): jnp.einsum('hqk,khd->hqd', weights.astype(jnp.bfloat16), values, preferre...  73.3 us
    dot_general x8, matrix products, attend_block(): jnp.einsum('qhd,khd->hqk', queries, keys, preferred_element_type=jnp.floa...  68.5 us
    all_gather x1, waiting for transfers between devices, per_device(): key_piece = lax.all_gather(key, 'seq', axis=0, tiled=True)  39.5 us
    all_gather x1, waiting for transfers between devices, per_device(): value_piece = lax.all_gather(value, 'seq', axis=0, tiled=True)  39.2 us
  transfers between devices with their start and end apart: 4, of which 4 were waited for; matrix products, arithmetic and copies ran while one was open for 0% of the time, Pallas kernels for 0%

profile of v1, /device:TPU:0, one launch (start us, length us, event | category | flops | bytes accessed | tf_op | source)
XLA Modules:
  0.0 652.6 jit_solution(15249648961055495076)
XLA Ops:
  11.1 6.1 copy.13
  24.9 39.2 %all-gather.7.cloned.1.call-done = bf16[5760,384]{1,0:T(8,128)(2,1)} async-done(((bf16[720,384]{1,0:T(8,128)(2,1)}), bf16[5760,384]{1,0:T(8,128)(2,1)}) %all-gather.7.cloned.1.call-update) | async-done | bytes 4423696 | tf_op jit(solution)/shard_map/all_gather | solution.py:55
  64.0 39.5 %all-gather.5.cloned.1.call-done = bf16[5760,384]{1,0:T(8,128)(2,1)} async-done(((bf16[720,384]{1,0:T(8,128)(2,1)}), bf16[5760,384]{1,0:T(8,128)(2,1)}) %all-gather.5.cloned.1.call-update) | async-done | bytes 4423696 | tf_op jit(solution)/shard_map/all_gather | solution.py:54
  103.5 264.1 %while.18 = (s32[]{:T(128)}, f32[8,720]{1,0:T(8,128)}, f32[8,720]{1,0:T(8,128)}, f32[8,720,48]{1,2,0:T(8,128)}, bf16[5760,384]{1,0:T(8,128)(2,1)}, /*index=5*/bf...) while((s32[]{:T(128)}, f32[8,720]{1,0:T(8,128)}, ...), condition=%wide.region_5.0_spmd.clone, body=%wide.region_2.0_spmd.clone.sunk | while | flops 830298240 | bytes 67369216 | solution.py:67
  105.3 8.6 %bitcast_reduce_fusion.2 = (f32[8,720]{1,0:T(8,128)S(1)}, f32[8,720,720]{2,1,0:T(8,128)}) fusion(bf16[720,8,48]{0,2,1:T(8,128)(2,1)S(1)} %bitcast.45, bf16[720,8,48]{0,2,1:T(8,128)(2,1)S(1)} %get-tuple-element.275), kind=kOutput, calls=%fused_computation.1.clone.1 | convolution fusion | flops 406419840 | bytes 17717760 | tf_op jit(solution)/shard_map/while/body/eval_jaxpr/qhd,khd->hqk/dot_general | solution.py:21
  114.5 9.7 %fusion.56 = f32[8,720]{1,0:T(8,128)} fusion(f32[8,720,720]{2,1,0:T(8,128)} %get-tuple-element.244, f32[8,720]{1,0:T(8,128)} %select_maximum_fusion.2), kind=kLoop, calls=%fused_computation.4.clone.1 | loop fusion | flops 12435840 | bytes 16634880 | tf_op jit(solution)/shard_map/while/body/eval_jaxpr/reduce_sum | solution.py:25
  125.6 9.2 %fusion.58 = f32[8,720,48]{1,2,0:T(8,128)S(1)} fusion(bf16[720,8,48]{0,2,1:T(8,128)(2,1)S(1)} %bitcast.44, f32[8,720,720]{2,1,0:T(8,128)} %get-tuple-element.244, f32[8,720]{1,0:T(8,128)} %select_maximum_fusion.2, f32[8,720,48]{1,2,0:T(8,128)S(1)} %copy-done.3, f32[8,720]{1,0:T(8,128)S(1)} %get-tuple-element.247, pred[]{:T(512)S(6)} %compare.3), kind=kOutput, calls=%fused_computation.6.clone.1 | convolution fusion | flops 411402240 | bytes 19399680 | tf_op jit(solution)/shard_map/while/body/eval_jaxpr/hqk,khd->hqd/dot_general | solution.py:26
  137.7 8.6 %bitcast_reduce_fusion.2 = (f32[8,720]{1,0:T(8,128)S(1)}, f32[8,720,720]{2,1,0:T(8,128)}) fusion(bf16[720,8,48]{0,2,1:T(8,128)(2,1)S(1)} %bitcast.45, bf16[720,8,48]{0,2,1:T(8,128)(2,1)S(1)} %get-tuple-element.275), kind=kOutput, calls=%fused_computation.1.clone.1 | convolution fusion | flops 406419840 | bytes 17717760 | tf_op jit(solution)/shard_map/while/body/eval_jaxpr/qhd,khd->hqk/dot_general | solution.py:21
  147.6 9.7 %fusion.56 = f32[8,720]{1,0:T(8,128)} fusion(f32[8,720,720]{2,1,0:T(8,128)} %get-tuple-element.244, f32[8,720]{1,0:T(8,128)} %select_maximum_fusion.2), kind=kLoop, calls=%fused_computation.4.clone.1 | loop fusion | flops 12435840 | bytes 16634880 | tf_op jit(solution)/shard_map/while/body/eval_jaxpr/reduce_sum | solution.py:25
  158.7 9.2 %fusion.58 = f32[8,720,48]{1,2,0:T(8,128)S(1)} fusion(bf16[720,8,48]{0,2,1:T(8,128)(2,1)S(1)} %bitcast.44, f32[8,720,720]{2,1,0:T(8,128)} %get-tuple-element.244, f32[8,720]{1,0:T(8,128)} %select_maximum_fusion.2, f32[8,720,48]{1,2,0:T(8,128)S(1)} %copy-done.3, f32[8,720]{1,0:T(8,128)S(1)} %get-tuple-element.247, pred[]{:T(512)S(6)} %compare.3), kind=kOutput, calls=%fused_computation.6.clone.1 | convolution fusion | flops 411402240 | bytes 19399680 | tf_op jit(solution)/shard_map/while/body/eval_jaxpr/hqk,khd->hqd/dot_general | solution.py:26
  170.8 8.6 %bitcast_reduce_fusion.2 = (f32[8,720]{1,0:T(8,128)S(1)}, f32[8,720,720]{2,1,0:T(8,128)}) fusion(bf16[720,8,48]{0,2,1:T(8,128)(2,1)S(1)} %bitcast.45, bf16[720,8,48]{0,2,1:T(8,128)(2,1)S(1)} %get-tuple-element.275), kind=kOutput, calls=%fused_computation.1.clone.1 | convolution fusion | flops 406419840 | bytes 17717760 | tf_op jit(solution)/shard_map/while/body/eval_jaxpr/qhd,khd->hqk/dot_general | solution.py:21
  180.7 9.7 %fusion.56 = f32[8,720]{1,0:T(8,128)} fusion(f32[8,720,720]{2,1,0:T(8,128)} %get-tuple-element.244, f32[8,720]{1,0:T(8,128)} %select_maximum_fusion.2), kind=kLoop, calls=%fused_computation.4.clone.1 | loop fusion | flops 12435840 | bytes 16634880 | tf_op jit(solution)/shard_map/while/body/eval_jaxpr/reduce_sum | solution.py:25
  191.9 9.2 %fusion.58 = f32[8,720,48]{1,2,0:T(8,128)S(1)} fusion(bf16[720,8,48]{0,2,1:T(8,128)(2,1)S(1)} %bitcast.44, f32[8,720,720]{2,1,0:T(8,128)} %get-tuple-element.244, f32[8,720]{1,0:T(8,128)} %select_maximum_fusion.2, f32[8,720,48]{1,2,0:T(8,128)S(1)} %copy-done.3, f32[8,720]{1,0:T(8,128)S(1)} %get-tuple-element.247, pred[]{:T(512)S(6)} %compare.3), kind=kOutput, calls=%fused_computation.6.clone.1 | convolution fusion | flops 411402240 | bytes 19399680 | tf_op jit(solution)/shard_map/while/body/eval_jaxpr/hqk,khd->hqd/dot_general | solution.py:26
  203.9 8.6 %bitcast_reduce_fusion.2 = (f32[8,720]{1,0:T(8,128)S(1)}, f32[8,720,720]{2,1,0:T(8,128)}) fusion(bf16[720,8,48]{0,2,1:T(8,128)(2,1)S(1)} %bitcast.45, bf16[720,8,48]{0,2,1:T(8,128)(2,1)S(1)} %get-tuple-element.275), kind=kOutput, calls=%fused_computation.1.clone.1 | convolution fusion | flops 406419840 | bytes 17717760 | tf_op jit(solution)/shard_map/while/body/eval_jaxpr/qhd,khd->hqk/dot_general | solution.py:21
  213.8 9.7 %fusion.56 = f32[8,720]{1,0:T(8,128)} fusion(f32[8,720,720]{2,1,0:T(8,128)} %get-tuple-element.244, f32[8,720]{1,0:T(8,128)} %select_maximum_fusion.2), kind=kLoop, calls=%fused_computation.4.clone.1 | loop fusion | flops 12435840 | bytes 16634880 | tf_op jit(solution)/shard_map/while/body/eval_jaxpr/reduce_sum | solution.py:25
  225.0 9.2 %fusion.58 = f32[8,720,48]{1,2,0:T(8,128)S(1)} fusion(bf16[720,8,48]{0,2,1:T(8,128)(2,1)S(1)} %bitcast.44, f32[8,720,720]{2,1,0:T(8,128)} %get-tuple-element.244, f32[8,720]{1,0:T(8,128)} %select_maximum_fusion.2, f32[8,720,48]{1,2,0:T(8,128)S(1)} %copy-done.3, f32[8,720]{1,0:T(8,128)S(1)} %get-tuple-element.247, pred[]{:T(512)S(6)} %compare.3), kind=kOutput, calls=%fused_computation.6.clone.1 | convolution fusion | flops 411402240 | bytes 19399680 | tf_op jit(solution)/shard_map/while/body/eval_jaxpr/hqk,khd->hqd/dot_general | solution.py:26
  237.0 8.6 %bitcast_reduce_fusion.2 = (f32[8,720]{1,0:T(8,128)S(1)}, f32[8,720,720]{2,1,0:T(8,128)}) fusion(bf16[720,8,48]{0,2,1:T(8,128)(2,1)S(1)} %bitcast.45, bf16[720,8,48]{0,2,1:T(8,128)(2,1)S(1)} %get-tuple-element.275), kind=kOutput, calls=%fused_computation.1.clone.1 | convolution fusion | flops 406419840 | bytes 17717760 | tf_op jit(solution)/shard_map/while/body/eval_jaxpr/qhd,khd->hqk/dot_general | solution.py:21
  246.9 9.7 %fusion.56 = f32[8,720]{1,0:T(8,128)} fusion(f32[8,720,720]{2,1,0:T(8,128)} %get-tuple-element.244, f32[8,720]{1,0:T(8,128)} %select_maximum_fusion.2), kind=kLoop, calls=%fused_computation.4.clone.1 | loop fusion | flops 12435840 | bytes 16634880 | tf_op jit(solution)/shard_map/while/body/eval_jaxpr/reduce_sum | solution.py:25
  258.1 9.2 %fusion.58 = f32[8,720,48]{1,2,0:T(8,128)S(1)} fusion(bf16[720,8,48]{0,2,1:T(8,128)(2,1)S(1)} %bitcast.44, f32[8,720,720]{2,1,0:T(8,128)} %get-tuple-element.244, f32[8,720]{1,0:T(8,128)} %select_maximum_fusion.2, f32[8,720,48]{1,2,0:T(8,128)S(1)} %copy-done.3, f32[8,720]{1,0:T(8,128)S(1)} %get-tuple-element.247, pred[]{:T(512)S(6)} %compare.3), kind=kOutput, calls=%fused_computation.6.clone.1 | convolution fusion | flops 411402240 | bytes 19399680 | tf_op jit(solution)/shard_map/while/body/eval_jaxpr/hqk,khd->hqd/dot_general | solution.py:26
  270.1 8.6 %bitcast_reduce_fusion.2 = (f32[8,720]{1,0:T(8,128)S(1)}, f32[8,720,720]{2,1,0:T(8,128)}) fusion(bf16[720,8,48]{0,2,1:T(8,128)(2,1)S(1)} %bitcast.45, bf16[720,8,48]{0,2,1:T(8,128)(2,1)S(1)} %get-tuple-element.275), kind=kOutput, calls=%fused_computation.1.clone.1 | convolution fusion | flops 406419840 | bytes 17717760 | tf_op jit(solution)/shard_map/while/body/eval_jaxpr/qhd,khd->hqk/dot_general | solution.py:21
  280.0 9.7 %fusion.56 = f32[8,720]{1,0:T(8,128)} fusion(f32[8,720,720]{2,1,0:T(8,128)} %get-tuple-element.244, f32[8,720]{1,0:T(8,128)} %select_maximum_fusion.2), kind=kLoop, calls=%fused_computation.4.clone.1 | loop fusion | flops 12435840 | bytes 16634880 | tf_op jit(solution)/shard_map/while/body/eval_jaxpr/reduce_sum | solution.py:25
  291.2 9.2 %fusion.58 = f32[8,720,48]{1,2,0:T(8,128)S(1)} fusion(bf16[720,8,48]{0,2,1:T(8,128)(2,1)S(1)} %bitcast.44, f32[8,720,720]{2,1,0:T(8,128)} %get-tuple-element.244, f32[8,720]{1,0:T(8,128)} %select_maximum_fusion.2, f32[8,720,48]{1,2,0:T(8,128)S(1)} %copy-done.3, f32[8,720]{1,0:T(8,128)S(1)} %get-tuple-element.247, pred[]{:T(512)S(6)} %compare.3), kind=kOutput, calls=%fused_computation.6.clone.1 | convolution fusion | flops 411402240 | bytes 19399680 | tf_op jit(solution)/shard_map/while/body/eval_jaxpr/hqk,khd->hqd/dot_general | solution.py:26
  303.2 8.6 %bitcast_reduce_fusion.2 = (f32[8,720]{1,0:T(8,128)S(1)}, f32[8,720,720]{2,1,0:T(8,128)}) fusion(bf16[720,8,48]{0,2,1:T(8,128)(2,1)S(1)} %bitcast.45, bf16[720,8,48]{0,2,1:T(8,128)(2,1)S(1)} %get-tuple-element.275), kind=kOutput, calls=%fused_computation.1.clone.1 | convolution fusion | flops 406419840 | bytes 17717760 | tf_op jit(solution)/shard_map/while/body/eval_jaxpr/qhd,khd->hqk/dot_general | solution.py:21
  313.1 9.7 %fusion.56 = f32[8,720]{1,0:T(8,128)} fusion(f32[8,720,720]{2,1,0:T(8,128)} %get-tuple-element.244, f32[8,720]{1,0:T(8,128)} %select_maximum_fusion.2), kind=kLoop, calls=%fused_computation.4.clone.1 | loop fusion | flops 12435840 | bytes 16634880 | tf_op jit(solution)/shard_map/while/body/eval_jaxpr/reduce_sum | solution.py:25
  324.3 9.2 %fusion.58 = f32[8,720,48]{1,2,0:T(8,128)S(1)} fusion(bf16[720,8,48]{0,2,1:T(8,128)(2,1)S(1)} %bitcast.44, f32[8,720,720]{2,1,0:T(8,128)} %get-tuple-element.244, f32[8,720]{1,0:T(8,128)} %select_maximum_fusion.2, f32[8,720,48]{1,2,0:T(8,128)S(1)} %copy-done.3, f32[8,720]{1,0:T(8,128)S(1)} %get-tuple-element.247, pred[]{:T(512)S(6)} %compare.3), kind=kOutput, calls=%fused_computation.6.clone.1 | convolution fusion | flops 411402240 | bytes 19399680 | tf_op jit(solution)/shard_map/while/body/eval_jaxpr/hqk,khd->hqd/dot_general | solution.py:26
  336.3 8.6 %bitcast_reduce_fusion.2 = (f32[8,720]{1,0:T(8,128)S(1)}, f32[8,720,720]{2,1,0:T(8,128)}) fusion(bf16[720,8,48]{0,2,1:T(8,128)(2,1)S(1)} %bitcast.45, bf16[720,8,48]{0,2,1:T(8,128)(2,1)S(1)} %get-tuple-element.275), kind=kOutput, calls=%fused_computation.1.clone.1 | convolution fusion | flops 406419840 | bytes 17717760 | tf_op jit(solution)/shard_map/while/body/eval_jaxpr/qhd,khd->hqk/dot_general | solution.py:21
  346.2 9.7 %fusion.56 = f32[8,720]{1,0:T(8,128)} fusion(f32[8,720,720]{2,1,0:T(8,128)} %get-tuple-element.244, f32[8,720]{1,0:T(8,128)} %select_maximum_fusion.2), kind=kLoop, calls=%fused_computation.4.clone.1 | loop fusion | flops 12435840 | bytes 16634880 | tf_op jit(solution)/shard_map/while/body/eval_jaxpr/reduce_sum | solution.py:25
  357.4 9.2 %fusion.58 = f32[8,720,48]{1,2,0:T(8,128)S(1)} fusion(bf16[720,8,48]{0,2,1:T(8,128)(2,1)S(1)} %bitcast.44, f32[8,720,720]{2,1,0:T(8,128)} %get-tuple-element.244, f32[8,720]{1,0:T(8,128)} %select_maximum_fusion.2, f32[8,720,48]{1,2,0:T(8,128)S(1)} %copy-done.3, f32[8,720]{1,0:T(8,128)S(1)} %get-tuple-element.247, pred[]{:T(512)S(6)} %compare.3), kind=kOutput, calls=%fused_computation.6.clone.1 | convolution fusion | flops 411402240 | bytes 19399680 | tf_op jit(solution)/shard_map/while/body/eval_jaxpr/hqk,khd->hqd/dot_general | solution.py:26
  372.0 90.0 %all-reduce.2.cloned.1.call-done = bf16[720,1536]{1,0:T(8,128)(2,1)} async-done(((bf16[720,1536]{1,0:T(8,128)(2,1)}), bf16[720,1536]{1,0:T(8,128)(2,1)}) %all-reduce.2.cloned.1.call-update) | async-done | bytes 2211856 | tf_op jit(solution)/shard_map/psum | solution.py:71
  465.4 12.9 %convolution_convert_fusion = bf16[720,1536]{1,0:T(8,128)(2,1)} fusion(bf16[1536,1536]{1,0:T(8,128)(2,1)} %param.15, bf16[1536,1536]{1,0:T(8,128)(2,1)} %param.14, bf16[720,1536]{1,0:T(8,128)(2,1)} %all-reduce.2.cloned.1.call-done, bf16[720,1536]{1,0:T(8,128)(2,1)S(1)} %copy-done.2, f32[1536]{0:T(1024)S(1)} %copy-done.8, f32[720]{0:T(1024)S(1)} %add_rsqrt_fusion, ...), kind=kOutput, calls=%fused_computation.36 | convolution fusion | flops 6813573120 | bytes 16084608 | tf_op jit(solution)/shard_map/dot_general | solution.py:76
  478.4 156.3 %all-gather.9.cloned.1.call-done = bf16[2880,1536]{1,0:T(8,128)(2,1)} async-done(((bf16[720,1536]{1,0:T(8,128)(2,1)}), bf16[2880,1536]{1,0:T(8,128)(2,1)}) %all-gather.9.cloned.1.call-update) | async-done | bytes 8847376 | tf_op jit(solution)/shard_map/all_gather | solution.py:79
  634.7 6.9 %reduce_sum.65 = bf16[720,1536]{1,0:T(8,128)(2,1)} reduce(bf16[4,720,1536]{2,1,0:T(8,128)(2,1)} %bitcast.47, bf16[]{:T(256)} %constant.71.clone.1), dimensions={0}, to_apply=%region_9.0 | reduce | flops 3317760 | bytes 11059202 | tf_op jit(solution)/shard_map/reduce_sum | solution.py:79
  (133 shorter events, 68.5 us)
Async XLA Ops:
  6.5 362.4 %copy-start = (bf16[384,1536]{1,0:T(8,128)(2,1)S(1)}, bf16[384,1536]{1,0:T(8,128)(2,1)}, u32[]{:S(2)}) copy-start(bf16[384,1536]{1,0:T(8,128)(2,1)} %param.12) | copy-start | bytes 3538948
  6.5 57.5 %all-gather.7.cloned.1.call-start = ((), (), s32[]{:S(2)}) async-start(), calls=%async_computation.1 | async-start | bytes 4976640 | tf_op jit(solution)/shard_map/all_gather | solution.py:55
  8.6 8.6 %copy-start.1 = (bf16[720,1536]{1,0:T(8,128)(2,1)S(1)}, bf16[720,1536]{1,0:T(8,128)(2,1)}, u32[]{:S(2)}) copy-start(bf16[720,1536]{1,0:T(8,128)(2,1)} %param.9) | copy-start | bytes 6635524
  8.6 8.6 %copy-start.7 = (f32[1536]{0:T(1024)S(1)}, f32[1536]{0:T(1024)}, u32[]{:S(2)}) copy-start(f32[1536]{0:T(1024)} %param.10) | copy-start | bytes 18436
  23.6 79.9 %all-gather.5.cloned.1.call-start = ((), (), s32[]{:S(2)}) async-start(), calls=%async_computation | async-start | bytes 4976640 | tf_op jit(solution)/shard_map/all_gather | solution.py:54
  24.3 437.7 %all-reduce.2.cloned.1.call-start = ((), (), s32[]{:S(2)}) async-start(), calls=%async_computation.2 | async-start | bytes 4423680 | tf_op jit(solution)/shard_map/psum | solution.py:71
  114.5 11.1 %copy-start.3 = (f32[8,720,48]{1,2,0:T(8,128)S(1)}, f32[8,720,48]{1,2,0:T(8,128)}, u32[]{:S(2)}) copy-start(f32[8,720,48]{1,2,0:T(8,128)} %get-tuple-element.262) | copy-start | bytes 3317764 | tf_op jit(solution)/shard_map/while
  125.6 9.2 %copy-start.6 = (f32[8,720]{1,0:T(8,128)S(1)}, f32[8,720]{1,0:T(8,128)}, u32[]{:S(2)}) copy-start(f32[8,720]{1,0:T(8,128)} %select_maximum_fusion.2) | copy-start | bytes 69124 | tf_op jit(solution)/shard_map/while
  134.8 1.0 copy-start.4
  147.6 11.2 %copy-start.3 = (f32[8,720,48]{1,2,0:T(8,128)S(1)}, f32[8,720,48]{1,2,0:T(8,128)}, u32[]{:S(2)}) copy-start(f32[8,720,48]{1,2,0:T(8,128)} %get-tuple-element.262) | copy-start | bytes 3317764 | tf_op jit(solution)/shard_map/while
  158.7 9.2 %copy-start.6 = (f32[8,720]{1,0:T(8,128)S(1)}, f32[8,720]{1,0:T(8,128)}, u32[]{:S(2)}) copy-start(f32[8,720]{1,0:T(8,128)} %select_maximum_fusion.2) | copy-start | bytes 69124 | tf_op jit(solution)/shard_map/while
  167.9 1.0 copy-start.4
  180.7 11.2 %copy-start.3 = (f32[8,720,48]{1,2,0:T(8,128)S(1)}, f32[8,720,48]{1,2,0:T(8,128)}, u32[]{:S(2)}) copy-start(f32[8,720,48]{1,2,0:T(8,128)} %get-tuple-element.262) | copy-start | bytes 3317764 | tf_op jit(solution)/shard_map/while
  191.8 9.2 %copy-start.6 = (f32[8,720]{1,0:T(8,128)S(1)}, f32[8,720]{1,0:T(8,128)}, u32[]{:S(2)}) copy-start(f32[8,720]{1,0:T(8,128)} %select_maximum_fusion.2) | copy-start | bytes 69124 | tf_op jit(solution)/shard_map/while
  213.8 11.2 %copy-start.3 = (f32[8,720,48]{1,2,0:T(8,128)S(1)}, f32[8,720,48]{1,2,0:T(8,128)}, u32[]{:S(2)}) copy-start(f32[8,720,48]{1,2,0:T(8,128)} %get-tuple-element.262) | copy-start | bytes 3317764 | tf_op jit(solution)/shard_map/while
  225.0 9.2 %copy-start.6 = (f32[8,720]{1,0:T(8,128)S(1)}, f32[8,720]{1,0:T(8,128)}, u32[]{:S(2)}) copy-start(f32[8,720]{1,0:T(8,128)} %select_maximum_fusion.2) | copy-start | bytes 69124 | tf_op jit(solution)/shard_map/while
  246.9 11.2 %copy-start.3 = (f32[8,720,48]{1,2,0:T(8,128)S(1)}, f32[8,720,48]{1,2,0:T(8,128)}, u32[]{:S(2)}) copy-start(f32[8,720,48]{1,2,0:T(8,128)} %get-tuple-element.262) | copy-start | bytes 3317764 | tf_op jit(solution)/shard_map/while
  258.1 9.2 %copy-start.6 = (f32[8,720]{1,0:T(8,128)S(1)}, f32[8,720]{1,0:T(8,128)}, u32[]{:S(2)}) copy-start(f32[8,720]{1,0:T(8,128)} %select_maximum_fusion.2) | copy-start | bytes 69124 | tf_op jit(solution)/shard_map/while
  267.2 1.0 copy-start.4
  280.0 11.2 %copy-start.3 = (f32[8,720,48]{1,2,0:T(8,128)S(1)}, f32[8,720,48]{1,2,0:T(8,128)}, u32[]{:S(2)}) copy-start(f32[8,720,48]{1,2,0:T(8,128)} %get-tuple-element.262) | copy-start | bytes 3317764 | tf_op jit(solution)/shard_map/while
  291.2 9.2 %copy-start.6 = (f32[8,720]{1,0:T(8,128)S(1)}, f32[8,720]{1,0:T(8,128)}, u32[]{:S(2)}) copy-start(f32[8,720]{1,0:T(8,128)} %select_maximum_fusion.2) | copy-start | bytes 69124 | tf_op jit(solution)/shard_map/while
  300.4 1.0 copy-start.4
  313.1 11.2 %copy-start.3 = (f32[8,720,48]{1,2,0:T(8,128)S(1)}, f32[8,720,48]{1,2,0:T(8,128)}, u32[]{:S(2)}) copy-start(f32[8,720,48]{1,2,0:T(8,128)} %get-tuple-element.262) | copy-start | bytes 3317764 | tf_op jit(solution)/shard_map/while
  324.3 9.2 %copy-start.6 = (f32[8,720]{1,0:T(8,128)S(1)}, f32[8,720]{1,0:T(8,128)}, u32[]{:S(2)}) copy-start(f32[8,720]{1,0:T(8,128)} %select_maximum_fusion.2) | copy-start | bytes 69124 | tf_op jit(solution)/shard_map/while
  333.5 1.0 copy-start.4
  346.2 11.2 %copy-start.3 = (f32[8,720,48]{1,2,0:T(8,128)S(1)}, f32[8,720,48]{1,2,0:T(8,128)}, u32[]{:S(2)}) copy-start(f32[8,720,48]{1,2,0:T(8,128)} %get-tuple-element.262) | copy-start | bytes 3317764 | tf_op jit(solution)/shard_map/while
  357.4 9.2 %copy-start.6 = (f32[8,720]{1,0:T(8,128)S(1)}, f32[8,720]{1,0:T(8,128)}, u32[]{:S(2)}) copy-start(f32[8,720]{1,0:T(8,128)} %select_maximum_fusion.2) | copy-start | bytes 69124 | tf_op jit(solution)/shard_map/while
  366.6 1.0 copy-start.4
  369.0 93.0 %copy-start.2 = (bf16[720,1536]{1,0:T(8,128)(2,1)S(1)}, bf16[720,1536]{1,0:T(8,128)(2,1)}, u32[]{:S(2)}) copy-start(bf16[720,1536]{1,0:T(8,128)(2,1)} %param.9) | copy-start | bytes 6635524
  371.7 93.7 %copy-start.8 = (f32[1536]{0:T(1024)S(1)}, f32[1536]{0:T(1024)}, u32[]{:S(2)}) copy-start(f32[1536]{0:T(1024)} %param.13) | copy-start | bytes 18436
  371.7 263.0 %all-gather.9.cloned.1.call-start = ((), (), s32[]{:S(2)}) async-start(), calls=%async_computation.3 | async-start | bytes 11059200 | tf_op jit(solution)/shard_map/all_gather | solution.py:79
  462.0 2.4 copy-start.5
  (2 other events, 2.0 us)
Sparse Core Ops, SparseCore 0:
  23.7 40.2 all-gather.6
  65.9 37.5 all-gather.4
  371.8 90.1 all-reduce.1
  478.5 156.1 all-gather.8
